TPU v7x, 32 devices: a whole 2x2x4 slice. The times are simulated.
32 devices in a mesh: order: 8 (over y, x, core), axial: 4 (over z).
Axes of the slice: x: 2, y: 2, z: 4, core: 2. Of those that a mesh axis runs over, the one named last changes fastest.
Arguments:
- coefficients: bfloat16 [4, 2, 1024, 8, 1024], P(None, None, 'order', 'axial'), may hold values from -0.005859375 to 0.005859375
- order_lists: int32 [1024], replicated, may hold values from 0 to 1023, as said below
- lengths: int32 [1024], replicated, may hold values from 128 to 1024, as said below
Outputs:
- advection: bfloat16 [3, 2, 1024, 8, 1024], P(None, None, 'order', 'axial')
Inputs may be any that keep to these rules, and one draw needn't show every extreme that they name: `order_lists`: a permutation of the orders 0 to 1023; the device with index j along order holds slots j * 128 to (j + 1) * 128 - 1 of coefficients and advection. lengths[m] minus (128 + ((1023 - m) * 768) // 1023) lies in 0 to 128.
All inputs are finite; a program needn't handle non-finite values.
Results may differ from a plain program's by a relative error of at most 0.0095.
Values may be sent and summed in bfloat16 or wider, within the bound.
A program may use at most 128 MiB of HBM per device.

v0:
```python
import math

import jax
import jax.numpy as jnp
from jax import lax
from jax.sharding import PartitionSpec as P

R = 1024


def with_halo(block, sides, width):
    for axis, dim in sides:
        count = lax.axis_size(axis)
        forward = [(i, i + 1) for i in range(count - 1)]
        forward.append((count - 1, 0))
        backward = [(target, source) for source, target in forward]
        low = lax.ppermute(
            lax.slice_in_dim(block, block.shape[dim] - width, None, axis=dim), axis, forward
        )
        high = lax.ppermute(lax.slice_in_dim(block, 0, width, axis=dim), axis, backward)
        block = jnp.concatenate([low, block, high], axis=dim)
    return block


def radial_tables(radius_count, mode_count):
    radius_ids = jnp.arange(radius_count, dtype=jnp.int32)
    mode_ids = jnp.arange(mode_count, dtype=jnp.int32)
    phases = mode_ids[None, :] * (2 * radius_ids[:, None] + 1) % (4 * radius_count)
    angles_rad = phases.astype(jnp.float32) * (math.pi / (2 * radius_count))
    synthesis = jnp.cos(angles_rad).astype(jnp.bfloat16)
    analysis = (jnp.cos(angles_rad.T) * math.sqrt(2.0 / radius_count)).astype(jnp.bfloat16)
    return (synthesis, analysis)


def azimuthal_tables(order_ids, point_count):
    points = jnp.arange(point_count, dtype=jnp.int32)
    phases = order_ids[..., None] * points % point_count
    angles_rad = phases.astype(jnp.float32) * (2.0 * math.pi / point_count)
    cosines = jnp.cos(angles_rad)
    sines = jnp.sin(angles_rad)
    weight = jnp.where(order_ids == 0, 1.0, 2.0).astype(jnp.float32)[..., None]
    forward = jnp.stack((weight * cosines, -weight * sines), axis=-3).astype(jnp.bfloat16)
    factor = math.sqrt(2.0 / point_count)
    inverse = jnp.stack((cosines * factor, -sines * factor), axis=-3).astype(jnp.bfloat16)
    return (forward, inverse)


def shards(coefficients, order_lists, lengths):
    field_count, part_count, slot_count, plane_count, mode_count = coefficients.shape
    order_count = order_lists.shape[0]
    point_count = 2 * order_count
    radius_count = R
    group_count = lax.axis_size("order")
    band_width = radius_count // group_count
    synthesis, analysis = radial_tables(radius_count, mode_count)
    owned_ids = lax.dynamic_slice_in_dim(
        order_lists, lax.axis_index("order") * slot_count, slot_count
    )
    catalog = jnp.arange(order_count, dtype=jnp.int32)
    own_lengths = jnp.sum(
        jnp.where(owned_ids[:, None] == catalog[None, :], lengths[None, :], 0), axis=1
    )
    retained = jnp.arange(mode_count, dtype=jnp.int32)[None, :] < own_lengths[:, None]
    masked = jnp.where(
        retained[None, None, :, None, :], coefficients, jnp.zeros((), coefficients.dtype)
    )
    radial = jnp.einsum("fcmzk,rk->frzcm", masked, synthesis, preferred_element_type=jnp.float32)
    radial = radial.astype(jnp.bfloat16).reshape(
        field_count, radius_count, plane_count * part_count * slot_count
    )
    forward, inverse = azimuthal_tables(order_lists.reshape(group_count, slot_count), point_count)
    received = lax.all_to_all(radial, "order", split_axis=1, concat_axis=2, tiled=True)
    item_count = received.shape[0]
    lattice = received.reshape(
        item_count, band_width, group_count, plane_count, part_count, slot_count
    )
    physical = jnp.einsum(
        "frizcm,icmj->fzrj", lattice, forward, preferred_element_type=jnp.float32
    ).astype(jnp.bfloat16)
    padded = with_halo(physical[:3], (("axial", 1),), 2)
    widened = padded.astype(jnp.float32)
    gradient = (
        8.0 * (widened[:, 3 : plane_count + 3] - widened[:, 1 : plane_count + 1])
        - (widened[:, 4 : plane_count + 4] - widened[:, 0:plane_count])
    ) / 12.0
    products = (physical[3].astype(jnp.float32)[None] * gradient).astype(jnp.bfloat16)
    spectral = jnp.einsum(
        "gzrj,icmj->grizcm", products, inverse, preferred_element_type=jnp.float32
    )
    spectral = spectral.astype(jnp.bfloat16).reshape(
        3, band_width, group_count * plane_count * part_count * slot_count
    )
    received = lax.all_to_all(spectral, "order", split_axis=2, concat_axis=1, tiled=True)
    item_count = received.shape[0]
    lattice = received.reshape(item_count, radius_count, plane_count, part_count, slot_count)
    result = jnp.einsum("grzcm,kr->gcmzk", lattice, analysis, preferred_element_type=jnp.float32)
    return jnp.where(retained[None, None, :, None, :], result, 0.0).astype(jnp.bfloat16)


def solution(mesh):
    placed = (P(None, None, "order", "axial", None), P(), P())
    return jax.shard_map(
        shards,
        mesh=mesh,
        in_specs=placed,
        out_specs=P(None, None, "order", "axial", None),
        check_vma=False,
    )
```

profile of v0, /device:TPU:0, one launch (start us, length us, event | category | flops | bytes accessed | tf_op | source)
XLA Modules:
  0.0 382.5 jit_solution(8791086650537149125)
XLA Ops:
  0.0 0.8 dynamic_slice.3
  0.8 0.9 select_reduce_fusion
  1.6 0.1 iota_compare_fusion.1
  1.8 0.2 copy.46
  2.0 9.3 %broadcast_select_fusion = bf16[4,2,128,2,1024]{4,3,2,1,0:T(2,128)(2,1)} fusion(bf16[4,2,128,2,1024]{4,3,2,1,0:T(2,128)(2,1)} %param.3, pred[128,1024]{1,0:T(8,128)(4,1)S(1)} %copy.46), kind=kLoop, calls=%fused_computation.22 | loop fusion | flops 2097152 | bytes 8519680 | tf_op jit(solution)/shard_map/jit(_where)/select_n | solution.py:64
  11.3 21.9 %convert_bitcast_fusion = bf16[4,1024,2,2,128]{1,4,2,3,0:T(8,128)(2,1)S(1)} fusion(bf16[4,2,128,2,1024]{4,3,2,1,0:T(2,128)(2,1)} %broadcast_select_fusion, s32[1024]{0:T(1024)S(1)} %multiply_add_fusion), kind=kOutput, calls=%fused_computation.51 | convolution fusion | flops 4312793088 | bytes 8392704 | tf_op jit(solution)/shard_map/fcmzk,rk->frzcm/dot_general | solution.py:67
  33.3 2.4 copy.48
  35.7 7.8 %copy.49 = bf16[4,1024,512]{2,0,1:T(4,128)(2,1)} copy(bf16[4,1024,512]{1,2,0:T(8,128)(2,1)} %bitcast.66) | data formatting | bytes 8388608 | tf_op jit(solution)/shard_map/reshape | solution.py:68
  43.5 0.0 copy-start.2
  43.5 5.6 %all-to-all-start = ((bf16[4,1024,512]{2,0,1:T(4,128)(2,1)}), bf16[4,1024,512]{2,0,1:T(4,128)(2,1)}, u32[]{:S(2)}, u32[]{:S(2)}) async-start(bf16[4,1024,512]{2,0,1:T(4,128)(2,1)} %copy.49), calls=%async_computation | async-start | bytes 8388608 | tf_op jit(solution)/shard_map/all_to_all | solution.py:72
  49.1 0.0 copy-done.2
  49.2 38.0 %multiply_convert_fusion.3 = (bf16[8,1,128,2048]{2,3,0,1:T(8,128)(2,1)}, bf16[8,1,128,2048]{2,3,0,1:T(8,128)(2,1)}, bf16[8,1,128,2048]{2,3,0,1:T(8,128)(2,1)}, bf16[8,1,128,2048]{2,3,0,1:T(8,128)(2,1)}) fusion(s32[8,128]{1,0:T(8,128)S(1)} %bitcast.71, f32[8,128]{1,0:T(8,128)S(1)} %get-tuple-element.9, f32[8,128]{1,0:T(8,128)S(1)} %get-tuple-element.10), kind=kLoop, calls=%fused_computation.18 | loop fusion | flops 48234496 | bytes 16789504 | tf_op jit(solution)/shard_map/convert.2
  87.2 11.1 %all-to-all-done = bf16[4,1024,512]{2,0,1:T(4,128)(2,1)} async-done(((bf16[4,1024,512]{2,0,1:T(4,128)(2,1)}), bf16[4,1024,512]{2,0,1:T(4,128)(2,1)}, u32[]{:S(2)}, u32[]{:S(2)}) %all-to-all-start) | async-done | bytes 4194336 | tf_op jit(solution)/shard_map/all_to_all | solution.py:72
  98.3 3.0 copy.50
  101.3 0.0 copy-start
  101.3 0.0 copy-start.1
  101.3 2.4 copy.51
  103.8 0.0 copy-done
  103.8 1.0 copy-done.1
  104.8 9.2 %fusion.38 = bf16[4,2,128,2048]{2,3,1,0:T(8,128)(2,1)S(1)} fusion(bf16[4,128,8,2,2,128]{5,2,4,3,1,0:T(8,128)(2,1)S(1)} %bitcast.70, bf16[8,1,128,2048]{2,3,0,1:T(8,128)(2,1)S(1)} %copy-done.1, bf16[8,1,128,2048]{2,3,0,1:T(8,128)(2,1)S(1)} %copy-done), kind=kOutput, calls=%fused_computation.60 | convolution fusion | flops 8608808960 | bytes 16777216 | tf_op jit(solution)/shard_map/frizcm,icmj->fzrj/dot_general | solution.py:77
  114.0 0.2 slice.24
  114.2 4.4 %collective-permute-start.1 = (bf16[3,2,128,2048]{2,3,1,0:T(8,128)(2,1)S(1)}, bf16[3,2,128,2048]{2,3,1,0:T(8,128)(2,1)S(1)}, u32[]{:S(2)}, u32[]{:S(2)}) collective-permute-start(bf16[3,2,128,2048]{2,3,1,0:T(8,128)(2,1)S(1)} %slice.24), channel_id=1, source_target_pairs={{1,0},{2,1},{3,2},{0,3},{5,4},{6,5},{7,6},{4,7},{9,8},{10,9},{11,1... | collective-permute-start | bytes 9437192 | tf_op jit(solution)/shard_map/ppermute | solution.py:20
  118.6 0.0 collective-permute-start
  118.6 1.5 multiply_bitcast_fusion
  120.1 67.0 %collective-permute-done.1 = bf16[3,2,128,2048]{2,3,1,0:T(8,128)(2,1)S(1)} collective-permute-done((bf16[3,2,128,2048]{2,3,1,0:T(8,128)(2,1)S(1)}, bf16[3,2,128,2048]{2,3,1,0:T(8,128)(2,1)S(1)}, u32[]{:S(2)}, u32[]{:S(2)}) %collective-permute-start.1) | collective-permute-done | bytes 3145760 | tf_op jit(solution)/shard_map/ppermute | solution.py:20
  187.1 64.2 %collective-permute-done = bf16[3,2,128,2048]{2,3,1,0:T(8,128)(2,1)S(1)} collective-permute-done((bf16[3,2,128,2048]{2,3,1,0:T(8,128)(2,1)S(1)}, bf16[3,2,128,2048]{2,3,1,0:T(8,128)(2,1)S(1)}, u32[]{:S(2)}, u32[]{:S(2)}) %collective-permute-start) | collective-permute-done | bytes 3145760 | tf_op jit(solution)/shard_map/ppermute | solution.py:17
  251.3 7.1 %maximum_convert_fusion = f32[3,6,128,2048]{2,3,1,0:T(8,128)} fusion(bf16[3,2,128,2048]{2,3,1,0:T(8,128)(2,1)S(1)} %collective-permute-done.1, bf16[3,2,128,2048]{2,3,1,0:T(8,128)(2,1)S(1)} %slice.24, bf16[3,2,128,2048]{2,3,1,0:T(8,128)(2,1)S(1)} %collective-permute-done), kind=kLoop, calls=%fused_computation.3 | loop fusion | flops 14155776 | bytes 28311552 | tf_op jit(solution)/shard_map/convert_element_type | solution.py:81
  258.4 18.2 %convert_bitcast_fusion.1 = bf16[3,128,8,2,2,128]{1,5,3,0,4,2:T(8,128)(2,1)S(1)} fusion(f32[2,128,2048]{1,2,0:T(8,128)} %multiply_bitcast_fusion, f32[3,6,128,2048]{2,3,1,0:T(8,128)} %maximum_convert_fusion, bf16[8,1,128,2048]{2,3,0,1:T(8,128)(2,1)} %get-tuple-element.7, bf16[8,1,128,2048]{2,3,0,1:T(8,128)(2,1)} %get-tuple-element.5), kind=kOutput, calls=%fused_computation.63 | convolution fusion | flops 6457655296 | bytes 38797312 | tf_op jit(solution)/shard_map/gzrj,icmj->grizcm/dot_general | solution.py:87
  276.6 0.2 copy.55
  276.8 20.0 %copy.56 = bf16[3,128,4096]{1,0,2:T(4,128)(2,1)S(1)} copy(bf16[3,128,4096]{1,2,0:T(8,128)(2,1)S(1)} %bitcast.68) | data formatting | bytes 6291456 | tf_op jit(solution)/shard_map/reshape | solution.py:90
  296.8 53.8 %all_to_all.30 = bf16[3,128,4096]{1,0,2:T(4,128)(2,1)S(1)} all-to-all(bf16[3,128,4096]{1,0,2:T(4,128)(2,1)S(1)} %copy.56), channel_id=1, replica_groups=mesh['order'=8,'axial'=4] {'order'}, dimensions={2} | all-to-all | bytes 6291456 | tf_op jit(solution)/shard_map/all_to_all | solution.py:93
  350.6 2.6 copy.83
  353.2 3.3 reshape.125
  356.5 20.2 %fusion.15 = bf16[3,2,128,2,1024]{2,4,1,3,0:T(8,128)(2,1)S(1)} fusion(pred[128,1024]{0,1:T(8,128)(4,1)S(1)} %iota_compare_fusion.1, bf16[3,1024,2,2,128]{1,4,3,2,0:T(8,128)(2,1)} %reshape.125, s32[1024]{0:T(1024)S(1)} %multiply_add_fusion), kind=kOutput, calls=%fused_computation.30 | convolution fusion | flops 3241148416 | bytes 6426624 | tf_op jit(solution)/shard_map/grzcm,kr->gcmzk/dot_general | solution.py:96
  376.7 5.6 %copy.59 = bf16[3,2,128,2,1024]{4,3,2,1,0:T(2,128)(2,1)} copy(bf16[3,2,128,2,1024]{2,4,1,3,0:T(8,128)(2,1)S(1)} %fusion.15) | data formatting | bytes 6291456 | tf_op jit(solution)/shard_map/convert_element_type | solution.py:97
  (2 shorter events, 0.0 us)
Async XLA Ops:
  43.5 5.6 %copy-start.2 = (s32[1024]{0:T(1024)S(1)}, s32[1024]{0:T(1024)}, u32[]{:S(2)}) copy-start(s32[1024]{0:T(1024)} %param.4) | copy-start | bytes 12292
  43.5 54.8 %all-to-all-start = ((bf16[4,1024,512]{2,0,1:T(4,128)(2,1)}), bf16[4,1024,512]{2,0,1:T(4,128)(2,1)}, u32[]{:S(2)}, u32[]{:S(2)}) async-start(bf16[4,1024,512]{2,0,1:T(4,128)(2,1)} %copy.49), calls=%async_computation | async-start | bytes 8388608 | tf_op jit(solution)/shard_map/all_to_all | solution.py:72
  101.3 2.4 copy-start
  101.3 3.5 copy-start.1
  114.2 72.9 %collective-permute-start.1 = (bf16[3,2,128,2048]{2,3,1,0:T(8,128)(2,1)S(1)}, bf16[3,2,128,2048]{2,3,1,0:T(8,128)(2,1)S(1)}, u32[]{:S(2)}, u32[]{:S(2)}) collective-permute-start(bf16[3,2,128,2048]{2,3,1,0:T(8,128)(2,1)S(1)} %slice.24), channel_id=1, source_target_pairs={{1,0},{2,1},{3,2},{0,3},{5,4},{6,5},{7,6},{4,7},{9,8},{10,9},{11,1... | collective-permute-start | bytes 9437192 | tf_op jit(solution)/shard_map/ppermute | solution.py:20
  118.6 132.7 %collective-permute-start = (bf16[3,2,128,2048]{2,3,1,0:T(8,128)(2,1)S(1)}, bf16[3,2,128,2048]{2,3,1,0:T(8,128)(2,1)S(1)}, u32[]{:S(2)}, u32[]{:S(2)}) collective-permute-start(bf16[3,2,128,2048]{2,3,1,0:T(8,128)(2,1)S(1)} %slice.24), channel_id=1, source_target_pairs={{0,1},{1,2},{2,3},{3,0},{4,5},{5,6},{6,7},{7,4},{8,9},{9,10},{10,1... | collective-permute-start | bytes 9437192 | tf_op jit(solution)/shard_map/ppermute | solution.py:17
where the time goes:
time: 388 us; the launch traced here: 382 us
  waiting for transfers between devices  142 us (37%)
  matrix products  69.5 us (18%)
  other arithmetic  56.9 us (15%)
  blocking collectives  53.8 us (14%)
  local copies, waits for them, and re-layouts  49.6 us (13%)
  starting transfers between devices  9.99 us (3%)
    ppermute x1, waiting for transfers between devices, with_halo(): lax.ppermute(lax.slice_in_dim(block, 0, width, axis=dim), axis, backward)  67 us
    ppermute x1, waiting for transfers between devices, with_halo(): lax.ppermute(lax.slice_in_dim(block, block.shape[dim] - width, None, axis...  64.2 us
    all_to_all x1, blocking collectives, shards(): lax.all_to_all(spectral, 'order', split_axis=2, concat_axis=1, tiled=True)  53.8 us
    another operation x1, other arithmetic  38 us
    dot_general x1, matrix products, shards(): jnp.einsum('fcmzk,rk->frzcm', masked, synthesis, preferred_element_type=j...  21.9 us
    dot_general x1, matrix products, shards(): jnp.einsum('grzcm,kr->gcmzk', lattice, analysis, preferred_element_type=j...  20.2 us
    reshape x1, local copies, waits for them, and re-layouts, shards(): spectral.astype(jnp.bfloat16)  20 us
    dot_general x1, matrix products, shards(): jnp.einsum('gzrj,icmj->grizcm', products, inverse, preferred_element_type...  18.2 us
  transfers between devices with their start and end apart: 3, of which 3 were waited for; matrix products, arithmetic and copies ran while one was open for 10% of the time, Pallas kernels for 0%

commit v1 on v0

v1 whole, which is shorter than its diff:
```python
import functools
import math

import jax
import jax.numpy as jnp
from jax import lax
from jax.experimental import pallas as pl
from jax.experimental.pallas import tpu as pltpu
from jax.sharding import PartitionSpec as P


R = 1024


def table_kernel(ca, sa, cb, sb, out):
    width = cb.shape[1]
    for h in range(ca.shape[1]):
        c0, s0 = ca[:, h : h + 1], sa[:, h : h + 1]
        cols = slice(h * width, (h + 1) * width)
        out[0, 0, :, cols] = (c0 * cb[...] - s0 * sb[...]).astype(out.dtype)
        if out.shape[1] > 1:
            out[0, 1, :, cols] = (-s0 * cb[...] - c0 * sb[...]).astype(out.dtype)


def wave_table(ids, groups, period, columns, kinds):
    count = ids.shape[0]
    rows = count // groups
    low = 128
    high = columns // low

    def parts(steps):
        angle = ((ids[:, None] * steps[None, :]) % period).astype(jnp.float32) * (
            2.0 * math.pi / period
        )
        return jnp.cos(angle), jnp.sin(angle)

    ca, sa = parts(jnp.arange(high, dtype=jnp.int32) * low)
    cb, sb = parts(jnp.arange(low, dtype=jnp.int32))
    spec_a = pl.BlockSpec((rows, high), lambda i: (i, 0))
    spec_b = pl.BlockSpec((rows, low), lambda i: (i, 0))
    return pl.pallas_call(
        table_kernel,
        grid=(groups,),
        in_specs=[spec_a, spec_a, spec_b, spec_b],
        out_specs=pl.BlockSpec((1, kinds, rows, columns), lambda i: (i, 0, 0, 0)),
        out_shape=jax.ShapeDtypeStruct((groups, kinds, rows, columns), jnp.bfloat16),
        cost_estimate=pl.CostEstimate(
            flops=6 * kinds * count * columns,
            bytes_accessed=2 * kinds * count * columns,
            transcendentals=0,
        ),
        name="wave_table",
    )(ca, sa, cb, sb).reshape(kinds * count, columns)


def gather_rows(x, xs, planes):
    groups, band, width = x.shape
    part = width // planes
    for i in range(groups):
        for z in range(planes):
            xs[z * band : (z + 1) * band, i * part : (i + 1) * part] = x[
                i, :, z * part : (z + 1) * part
            ]


def physical_kernel(planes, x, table, out, xs):
    @pl.when(pl.program_id(0) == 0)
    def _():
        gather_rows(x, xs, planes)

    out[...] = jnp.dot(xs[...], table[...], preferred_element_type=jnp.float32).astype(out.dtype)


def product_kernel(planes, factor, x, table, advecting, out, xs, total):
    step = pl.program_id(0)

    @pl.when(step == 0)
    def _():
        gather_rows(x, xs, planes)

    gradient = jnp.dot(xs[...], table[...], preferred_element_type=jnp.float32)
    products = (advecting[...].astype(jnp.float32) * gradient).astype(jnp.bfloat16)
    term = lax.dot_general(
        products, table[...], (((1,), (1,)), ((), ())), preferred_element_type=jnp.float32
    )

    @pl.when(step == 0)
    def _():
        total[...] = term

    @pl.when(step > 0)
    def _():
        total[...] += term

    @pl.when(step == pl.num_programs(0) - 1)
    def _():
        groups, band, width = out.shape
        part = width // planes
        for i in range(groups):
            for z in range(planes):
                out[i, :, z * part : (z + 1) * part] = (
                    total[z * band : (z + 1) * band, i * part : (i + 1) * part] * factor
                ).astype(out.dtype)


def call_physical(x, table, planes):
    groups, band, width = x.shape
    rows, depth, points = planes * band, table.shape[0], table.shape[1]
    tile = min(512, points)
    return pl.pallas_call(
        functools.partial(physical_kernel, planes),
        grid=(points // tile,),
        in_specs=[
            pl.BlockSpec((groups, band, width), lambda j: (0, 0, 0)),
            pl.BlockSpec((depth, tile), lambda j: (0, j)),
        ],
        out_specs=pl.BlockSpec((rows, tile), lambda j: (0, j)),
        out_shape=jax.ShapeDtypeStruct((rows, points), jnp.bfloat16),
        scratch_shapes=[pltpu.VMEM((rows, depth), jnp.bfloat16)],
        cost_estimate=pl.CostEstimate(
            flops=2 * rows * depth * points, bytes_accessed=2 * depth * points, transcendentals=0
        ),
        name="physical",
    )(x, table)


def call_products(x, table, advecting, planes, factor):
    groups, band, width = x.shape
    rows, depth, points = planes * band, table.shape[0], table.shape[1]
    tile = min(512, points)
    whole = pl.BlockSpec((groups, band, width), lambda j: (0, 0, 0))
    return pl.pallas_call(
        functools.partial(product_kernel, planes, factor),
        grid=(points // tile,),
        in_specs=[
            whole,
            pl.BlockSpec((depth, tile), lambda j: (0, j)),
            pl.BlockSpec((rows, tile), lambda j: (0, j)),
        ],
        out_specs=whole,
        out_shape=jax.ShapeDtypeStruct(x.shape, jnp.bfloat16),
        scratch_shapes=[
            pltpu.VMEM((rows, depth), jnp.bfloat16),
            pltpu.VMEM((rows, depth), jnp.float32),
        ],
        cost_estimate=pl.CostEstimate(
            flops=4 * rows * depth * points, bytes_accessed=2 * depth * points, transcendentals=0
        ),
        name="products",
    )(x, table, advecting)


def split_kernel(source, _, out):
    for c in range(out.shape[1]):
        value = source[0, c].astype(jnp.float32)
        for z in range(out.shape[0]):
            out[z, c] = value[:, z, :].astype(out.dtype)


def call_split(coefficients, field, after):
    _, parts, slots, planes, modes = coefficients.shape
    tile = min(256, modes)
    return pl.pallas_call(
        split_kernel,
        grid=(modes // tile,),
        in_specs=[
            pl.BlockSpec((1, parts, slots, planes, tile), lambda k: (field, 0, 0, 0, k)),
            pl.BlockSpec(memory_space=pl.ANY),
        ],
        out_specs=pl.BlockSpec((planes, parts, slots, tile), lambda k: (0, 0, 0, k)),
        out_shape=jax.ShapeDtypeStruct((planes, parts, slots, modes), coefficients.dtype),
        cost_estimate=pl.CostEstimate(
            flops=0, bytes_accessed=4 * parts * slots * planes * modes, transcendentals=0
        ),
        name="split",
    )(coefficients, after)


def radial_kernel(width, *refs):
    *sources, scale, synthesis, _, out = refs
    planes, parts, slots, _ = sources[0].shape if len(sources) == 1 else sources[1].shape
    groups, band, _ = out.shape

    def plane(z, c):
        if len(sources) == 1:
            return sources[0][z, c].astype(jnp.float32)
        low, own, high = sources
        if z < width:
            return low[z, c].astype(jnp.float32)
        if z < width + planes:
            return own[z - width, c].astype(jnp.float32)
        return high[z - width - planes, c].astype(jnp.float32)

    for z in range(planes):
        for c in range(parts):
            if len(sources) == 1:
                value = plane(z, c)
            else:
                value = (
                    8.0 * (plane(z + 3, c) - plane(z + 1, c)) - (plane(z + 4, c) - plane(z, c))
                ) / 12.0
            rows = (value * scale[...]).astype(jnp.bfloat16)
            first = (z * parts + c) * slots
            for i in range(groups):
                out[i, :, first : first + slots] = lax.dot_general(
                    synthesis[i * band : (i + 1) * band],
                    rows,
                    (((1,), (1,)), ((), ())),
                    preferred_element_type=jnp.float32,
                ).astype(out.dtype)


def call_radial(sources, scale, synthesis, after, groups, width):
    planes, parts, slots, modes = sources[len(sources) // 2].shape
    radii = synthesis.shape[0]
    columns = planes * parts * slots
    held = pl.BlockSpec(memory_space=pltpu.VMEM)
    return pl.pallas_call(
        functools.partial(radial_kernel, width),
        in_specs=[held] * (len(sources) + 2) + [pl.BlockSpec(memory_space=pl.ANY)],
        out_specs=held,
        out_shape=jax.ShapeDtypeStruct((groups, radii // groups, columns), jnp.bfloat16),
        cost_estimate=pl.CostEstimate(
            flops=2 * radii * columns * modes, bytes_accessed=8 * columns * modes, transcendentals=0
        ),
        name="radial",
    )(*sources, scale, synthesis, after)


def analysis_kernel(y, synthesis, kept, *refs):
    out = refs[-1]
    _, parts, slots, planes, _ = out.shape
    held = y[...].reshape(synthesis.shape[0], -1)
    for c in range(parts):
        rows = []
        for z in range(planes):
            first = (z * parts + c) * slots
            term = lax.dot_general(
                held[:, first : first + slots],
                synthesis[...],
                (((0,), (0,)), ((), ())),
                preferred_element_type=jnp.float32,
            )
            rows.append(term * kept[...])
        out[0, c] = jnp.stack(rows, axis=1).astype(out.dtype)


def call_analysis(y, synthesis, kept, field, shape, so_far):
    _, modes = synthesis.shape
    held = pl.BlockSpec(memory_space=pltpu.VMEM)
    more = () if so_far is None else (so_far,)
    return pl.pallas_call(
        analysis_kernel,
        grid=(1,),
        in_specs=[
            pl.BlockSpec(y.shape, lambda i: (0, 0, 0)),
            pl.BlockSpec(synthesis.shape, lambda i: (0, 0)),
            pl.BlockSpec(kept.shape, lambda i: (0, 0)),
        ]
        + [pl.BlockSpec(memory_space=pl.ANY)] * len(more),
        out_specs=pl.BlockSpec((1,) + shape[1:], lambda i: (field, 0, 0, 0, 0)),
        out_shape=jax.ShapeDtypeStruct(shape, jnp.bfloat16),
        input_output_aliases={3: 0} if more else {},
        cost_estimate=pl.CostEstimate(
            flops=2 * y.size * modes, bytes_accessed=4 * y.size, transcendentals=0
        ),
        name="analysis",
    )(y, synthesis, kept, *more)


def shards(coefficients, order_lists, lengths):
    field_count, part_count, slots, planes, modes = coefficients.shape
    order_count = order_lists.shape[0]
    points = 2 * order_count
    groups = lax.axis_size("order")
    axial = lax.axis_size("axial")
    width = 2
    onward = [(i, (i + 1) % axial) for i in range(axial)]
    backward = [(b, a) for a, b in onward]

    owns, halos = [], []
    after = order_lists
    for f in range(field_count):
        owns.append(call_split(coefficients, f, after))
        after = owns[f]
    for g in range(3):
        low = lax.ppermute(owns[g][planes - width :], "axial", onward)
        high = lax.ppermute(owns[g][:width], "axial", backward)
        halos.append((low, high))

    radius_ids = jnp.arange(R, dtype=jnp.int32)
    mode_ids = jnp.arange(modes, dtype=jnp.int32)
    synthesis = wave_table(2 * radius_ids + 1, groups, 4 * R, modes, 1)

    owned = lax.dynamic_slice_in_dim(order_lists, lax.axis_index("order") * slots, slots)
    catalog = jnp.arange(order_count, dtype=jnp.int32)
    own_lengths = jnp.sum(
        jnp.where(owned[:, None] == catalog[None, :], lengths[None, :], 0), axis=1
    )
    retained = mode_ids[None, :] < own_lengths[:, None]
    weight = jnp.where(owned == 0, 1.0, 2.0).astype(jnp.float32)[:, None]
    scale = jnp.where(retained, weight, 0.0)
    table = wave_table(order_lists, groups, points, points, 2)

    def exchange(x):
        return lax.all_to_all(x, "order", split_axis=0, concat_axis=0, tiled=True)

    first = call_radial((owns[3],), scale, synthesis, order_lists, groups, width)
    carried = exchange(first)
    advecting = call_physical(carried, table, planes)

    kept = jnp.where(retained, math.sqrt(2.0 / R), 0.0).astype(jnp.float32)
    after, result = carried, None
    for g in range(3):
        low, high = halos[g]
        radial = call_radial((low, owns[g], high), scale, synthesis, after, groups, width)
        arrived = exchange(radial)
        after = advecting if g == 0 else arrived
        products = call_products(
            arrived, table, advecting, planes, math.sqrt(2.0 / points)
        )
        spectral = exchange(products)
        shape = (3, part_count, slots, planes, modes)
        result = call_analysis(spectral, synthesis, kept, g, shape, result)
    return result


def solution(mesh):
    placed = (P(None, None, "order", "axial", None), P(), P())
    return jax.shard_map(
        shards,
        mesh=mesh,
        in_specs=placed,
        out_specs=P(None, None, "order", "axial", None),
        check_vma=False,
    )
```

time: 388 us -> 231 us (0.60); the launches traced: 382 us -> 229 us
  Pallas kernels: 0 us -> 113 us
  waiting for transfers between devices: 142 us -> 62.1 us
  matrix products: 69.5 us -> 0 us
  blocking collectives: 53.8 us -> 0 us
  local copies, waits for them, and re-layouts: 49.6 us -> 2.71 us
  other arithmetic: 56.9 us -> 14.2 us
  starting transfers between devices: 9.99 us -> 37 us
    pallas_call x0 -> x17, Pallas kernels: none -> 113 us  [the longest x3 28.1 us: call_products(): pl.pallas_call(functools.partial(product_kernel, planes, factor), grid=(p...]
    ppermute x2 -> x6, waiting for transfers between devices: 131 us -> 31.7 us  [the longest x3 24.9 us: shards(): low = lax.ppermute(owns[g][planes - width:], 'axial', onward)]
    dot_general x4 -> x0, matrix products: 69.5 us -> none  [the longest x1 21.9 us: shards(): jnp.einsum('fcmzk,rk->frzcm', masked, synthesis, preferred_element_type=j...]
    all_to_all x1 -> x0, blocking collectives: 53.8 us -> none  [shards(): lax.all_to_all(spectral, 'order', split_axis=2, concat_axis=1, tiled=True)]
    another operation x1 -> x0, other arithmetic: 38 us -> none
    reshape x3 -> x0, local copies, waits for them, and re-layouts: 31.2 us -> none  [the longest x1 20 us: shards(): spectral.astype(jnp.bfloat16)]
    all_to_all x1 -> x7, starting transfers between devices: 5.62 us -> 25.9 us  [exchange(): return lax.all_to_all(x, 'order', split_axis=0, concat_axis=0, tiled=True)]
    all_to_all x1 -> x7, waiting for transfers between devices: 11.1 us -> 30.5 us  [exchange(): return lax.all_to_all(x, 'order', split_axis=0, concat_axis=0, tiled=True)]
  transfers between devices with their start and end apart: 3 -> 13, of which waited for: 3 -> 8; matrix products, arithmetic and copies ran while one was open for 10% -> 6% of each run, Pallas kernels for 0% -> 45%
where the time goes in v1:
time: 231 us; the launch traced here: 229 us
  Pallas kernels  113 us (49%)
  waiting for transfers between devices  62.1 us (27%)
  starting transfers between devices  37 us (16%)
  other arithmetic  14.2 us (6%)
  local copies, waits for them, and re-layouts  2.71 us (1%)
    all_to_all x7, waiting for transfers between devices, exchange(): return lax.all_to_all(x, 'order', split_axis=0, concat_axis=0, tiled=True)  30.5 us
    pallas_call x3, Pallas kernels, call_products(): pl.pallas_call(functools.partial(product_kernel, planes, factor), grid=(p...  28.1 us
    all_to_all x7, starting transfers between devices, exchange(): return lax.all_to_all(x, 'order', split_axis=0, concat_axis=0, tiled=True)  25.9 us
    ppermute x3, waiting for transfers between devices, shards(): low = lax.ppermute(owns[g][planes - width:], 'axial', onward)  24.9 us
    pallas_call x4, Pallas kernels, call_radial(): pl.pallas_call(functools.partial(radial_kernel, width), in_specs=[held] *...  23.9 us
    pallas_call x4, Pallas kernels, call_split(): pl.pallas_call(split_kernel, grid=(modes // tile,), in_specs=[pl.BlockSpe...  19.4 us
    pallas_call x3, Pallas kernels, call_analysis(): pl.pallas_call(analysis_kernel, grid=(1,), in_specs=[pl.BlockSpec(y.shape...  17.9 us
    pallas_call x2, Pallas kernels, wave_table(): pl.pallas_call(table_kernel, grid=(groups,), in_specs=[spec_a, spec_a, sp...  17.3 us
  transfers between devices with their start and end apart: 13, of which 8 were waited for; matrix products, arithmetic and copies ran while one was open for 6% of the time, Pallas kernels for 45%

profile of v1, /device:TPU:0, one launch (start us, length us, event | category | flops | bytes accessed | tf_op | source)
XLA Modules:
  0.0 229.5 jit_solution(659776528580202803)
XLA Ops:
  0.0 4.8 %split.4._.refs_1_ = bf16[2,2,128,1024]{3,2,1,0:T(8,128)(2,1)} custom-call(bf16[4,2,128,2,1024]{4,3,2,1,0:T(2,128)(2,1)} %source.7, s32[1024]{0:T(1024)} %refs_3_.1), custom_call_target="tpu_custom_call" | custom-call | bytes 2097152 | tf_op jit(solution)/shard_map/split/pallas_call | solution.py:163
  4.8 5.1 %collective-permute-start.5 = (bf16[2,2,128,1024]{3,2,1,0:T(8,128)(2,1)}, bf16[2,2,128,1024]{3,2,1,0:T(8,128)(2,1)S(1)}, u32[]{:S(2)}, u32[]{:S(2)}) collective-permute-start(bf16[2,2,128,1024]{3,2,1,0:T(8,128)(2,1)} %split.4._.refs_1_), channel_id=1, source_target_pairs={{1,0},{2,1},{3,2},{0,3},{5,4},{6,5},{7,6},{4,7},{9,8},{10,9},{11,1... | collective-permute-start | bytes 3145736 | tf_op jit(solution)/shard_map/ppermute | solution.py:288
  9.9 0.0 collective-permute-start.4
  9.9 0.8 compare_select_fusion
  10.7 3.2 %fusion.16 = (f32[1024,128]{1,0:T(8,128)}, f32[1024,128]{1,0:T(8,128)}) fusion(s32[1024]{0:T(1024)S(1)} %multiply_add_fusion), kind=kLoop, calls=%fused_computation.29 | loop fusion | flops 1835008 | bytes 1052672 | tf_op jit(solution)/shard_map/sin | solution.py:35
  13.9 0.1 fusion.20
  14.0 0.2 copy.6
  14.2 2.8 %multiply_sine_fusion.1 = (f32[1024,8]{1,0:T(8,128)}, f32[1024,8]{1,0:T(8,128)}) fusion(f32[1024,8]{1,0:T(8,128)S(1)} %copy.6), kind=kLoop, calls=%fused_computation.25 | loop fusion | flops 8192 | bytes 98304 | tf_op jit(solution)/shard_map/sin | solution.py:35
  17.0 0.0 copy-done.11
  17.0 0.2 select_reduce_fusion
  17.2 1.1 fusion.10
  18.3 4.9 %split.5._.refs_1_ = bf16[2,2,128,1024]{3,2,1,0:T(8,128)(2,1)} custom-call(bf16[4,2,128,2,1024]{4,3,2,1,0:T(2,128)(2,1)} %source.7, bf16[2,2,128,1024]{3,2,1,0:T(8,128)(2,1)} %split.4._.refs_1_), custom_call_target="tpu_custom_call" | custom-call | bytes 2097152 | tf_op jit(solution)/shard_map/split/pallas_call | solution.py:163
  23.2 4.8 %split.6._.refs_1_ = bf16[2,2,128,1024]{3,2,1,0:T(8,128)(2,1)} custom-call(bf16[4,2,128,2,1024]{4,3,2,1,0:T(2,128)(2,1)} %source.7, bf16[2,2,128,1024]{3,2,1,0:T(8,128)(2,1)} %split.5._.refs_1_), custom_call_target="tpu_custom_call" | custom-call | bytes 2097152 | tf_op jit(solution)/shard_map/split/pallas_call | solution.py:163
  28.0 4.9 %split.7.refs_0_ = bf16[2,2,128,1024]{3,2,1,0:T(8,128)(2,1)} custom-call(bf16[4,2,128,2,1024]{4,3,2,1,0:T(2,128)(2,1)} %source.7, bf16[2,2,128,1024]{3,2,1,0:T(8,128)(2,1)} %split.6._.refs_1_), custom_call_target="tpu_custom_call" | custom-call | bytes 2097152 | tf_op jit(solution)/shard_map/split/pallas_call | solution.py:163
  32.9 6.9 %wave_table.2 = bf16[8,1,128,1024]{3,2,1,0:T(8,128)(2,1)} custom-call(f32[1024,8]{1,0:T(8,128)} %get-tuple-element.10.ca, f32[1024,8]{1,0:T(8,128)} %get-tuple-element.9.sa, f32[1024,128]{1,0:T(8,128)} %get-tuple-element.14.cb, f32[1024,128]{1,0:T(8,128)} %get-tuple-element.13.sb), custom_call_target="tpu_custom_call" | custom-call | flops 6291456 | bytes 2097152 | tf_op jit(solution)/shard_map/wave_table/pallas_call | solution.py:41
  39.8 5.5 %radial.4 = bf16[8,128,512]{2,1,0:T(8,128)(2,1)} custom-call(bf16[2,2,128,1024]{3,2,1,0:T(8,128)(2,1)} %split.7.refs_0_, f32[128,1024]{1,0:T(8,128)} %get-tuple-element.16.refs_1_.refs_3_, bf16[1024,1024]{1,0:T(8,128)(2,1)} %bitcast.2, s32[1024]{0:T(1024)} %refs_3_.1), custom_call_target="tpu_custom_call" | custom-call | flops 1073741824 | bytes 4194304 | tf_op jit(solution)/shard_map/radial/pallas_call | solution.py:218
  45.3 3.7 %all-to-all-start = ((bf16[8,128,512]{2,1,0:T(8,128)(2,1)}), bf16[8,128,512]{2,1,0:T(8,128)(2,1)S(1)}, u32[]{:S(2)}, u32[]{:S(2)}) async-start(bf16[8,128,512]{2,1,0:T(8,128)(2,1)} %radial.4), calls=%async_computation | async-start | bytes 2097152 | tf_op jit(solution)/shard_map/all_to_all | solution.py:306
  49.0 0.0 copy-done.2
  49.0 3.9 %collective-permute-start.3 = (bf16[2,2,128,1024]{3,2,1,0:T(8,128)(2,1)S(1)}, bf16[2,2,128,1024]{3,2,1,0:T(8,128)(2,1)}, u32[]{:S(2)}, u32[]{:S(2)}) collective-permute-start(bf16[2,2,128,1024]{3,2,1,0:T(8,128)(2,1)S(1)} %copy-done.2), channel_id=1, source_target_pairs={{1,0},{2,1},{3,2},{0,3},{5,4},{6,5},{7,6},{4,7},{9,8},{10,9},{11,1... | collective-permute-start | bytes 3145736 | tf_op jit(solution)/shard_map/ppermute | solution.py:288
  52.9 0.0 collective-permute-start.2
  52.9 11.5 %all-to-all-done.x.refs_5_ = bf16[8,128,512]{2,1,0:T(8,128)(2,1)S(1)} async-done(((bf16[8,128,512]{2,1,0:T(8,128)(2,1)}), bf16[8,128,512]{2,1,0:T(8,128)(2,1)S(1)}, u32[]{:S(2)}, u32[]{:S(2)}) %all-to-all-start) | async-done | bytes 1048608 | tf_op jit(solution)/shard_map/all_to_all | solution.py:306
  64.4 0.0 collective-permute-done.5.refs_2_
  64.4 0.0 collective-permute-done.4.refs_0_
  64.4 1.0 copy-done
  65.3 0.4 copy-done.7
  65.7 6.1 %radial.7 = bf16[8,128,512]{2,1,0:T(8,128)(2,1)} custom-call(bf16[2,2,128,1024]{3,2,1,0:T(8,128)(2,1)} %collective-permute-done.4.refs_0_, bf16[2,2,128,1024]{3,2,1,0:T(8,128)(2,1)} %split.4._.refs_1_, bf16[2,2,128,1024]{3,2,1,0:T(8,128)(2,1)} %copy-done.7, f32[128,1024]{1,0:T(8,128)} %get-tuple-element.16.refs_1_.refs_3_, bf16[1024,1024]{1,0:T(8,128)(2,1)} %bitcast.3, ...), custom_call_target="tpu_custom_call" | custom-call | flops 1073741824 | bytes 4194304 | tf_op jit(solution)/shard_map/radial/pallas_call | solution.py:218
  71.8 3.7 %all-to-all-start.5 = ((bf16[8,128,512]{2,1,0:T(8,128)(2,1)}), bf16[8,128,512]{2,1,0:T(8,128)(2,1)S(1)}, u32[]{:S(2)}, u32[]{:S(2)}) async-start(bf16[8,128,512]{2,1,0:T(8,128)(2,1)} %radial.7), calls=%async_computation.5 | async-start | bytes 2097152 | tf_op jit(solution)/shard_map/all_to_all | solution.py:306
  75.6 0.0 copy-done.10
  75.6 0.1 fusion.18
  75.7 0.2 copy.7
  75.9 3.2 %fusion.14 = (f32[1024,128]{1,0:T(8,128)}, f32[1024,128]{1,0:T(8,128)}) fusion(s32[1024]{0:T(1024)S(1)} %copy-done.10), kind=kLoop, calls=%fused_computation.27 | loop fusion | flops 1835008 | bytes 1052672 | tf_op jit(solution)/shard_map/sin | solution.py:35
  79.2 2.7 %multiply_sine_fusion = (f32[1024,16]{1,0:T(8,128)}, f32[1024,16]{1,0:T(8,128)}) fusion(f32[1024,16]{1,0:T(8,128)S(1)} %copy.7), kind=kLoop, calls=%fused_computation.23 | loop fusion | flops 16384 | bytes 196608 | tf_op jit(solution)/shard_map/sin | solution.py:35
  81.9 10.4 %wave_table.3 = bf16[8,2,128,2048]{3,2,1,0:T(8,128)(2,1)} custom-call(f32[1024,16]{1,0:T(8,128)} %get-tuple-element.8.ca, f32[1024,16]{1,0:T(8,128)} %get-tuple-element.7.sa, f32[1024,128]{1,0:T(8,128)} %get-tuple-element.12.cb, f32[1024,128]{1,0:T(8,128)} %get-tuple-element.11.sb), custom_call_target="tpu_custom_call" | custom-call | flops 25165824 | bytes 8388608 | tf_op jit(solution)/shard_map/wave_table/pallas_call | solution.py:41
  92.3 6.7 %physical.1.refs_5_.advecting = bf16[256,2048]{1,0:T(8,128)(2,1)} custom-call(bf16[8,128,512]{2,1,0:T(8,128)(2,1)} %copy-done, bf16[2048,2048]{1,0:T(8,128)(2,1)} %bitcast.9), custom_call_target="tpu_custom_call" | custom-call | flops 2147483648 | bytes 8388608 | tf_op jit(solution)/shard_map/physical/pallas_call | solution.py:110
  99.0 0.0 collective-permute-done.3.refs_2_
  99.0 2.0 collective-permute-done.2.refs_0_
  101.0 6.1 %radial.5 = bf16[8,128,512]{2,1,0:T(8,128)(2,1)} custom-call(bf16[2,2,128,1024]{3,2,1,0:T(8,128)(2,1)} %collective-permute-done.2.refs_0_, bf16[2,2,128,1024]{3,2,1,0:T(8,128)(2,1)} %split.5._.refs_1_, bf16[2,2,128,1024]{3,2,1,0:T(8,128)(2,1)} %collective-permute-done.3.refs_2_, f32[128,1024]{1,0:T(8,128)} %get-tuple-element.16.refs_1_.refs_3_, ...), custom_call_target="tpu_custom_call" | custom-call | flops 1073741824 | bytes 4194304 | tf_op jit(solution)/shard_map/radial/pallas_call | solution.py:218
  107.1 0.0 all-to-all-done.5.x
  107.2 3.7 %all-to-all-start.1 = ((bf16[8,128,512]{2,1,0:T(8,128)(2,1)}), bf16[8,128,512]{2,1,0:T(8,128)(2,1)S(1)}, u32[]{:S(2)}, u32[]{:S(2)}) async-start(bf16[8,128,512]{2,1,0:T(8,128)(2,1)} %radial.5), calls=%async_computation.1 | async-start | bytes 2097152 | tf_op jit(solution)/shard_map/all_to_all | solution.py:306
  110.9 0.0 copy-done.1
  110.9 2.1 collective-permute-start.1
  113.0 0.0 collective-permute-start
  113.0 0.0 copy-done.8
  113.0 9.4 %products.5 = bf16[8,128,512]{2,1,0:T(8,128)(2,1)} custom-call(bf16[8,128,512]{2,1,0:T(8,128)(2,1)} %copy-done.8, bf16[2048,2048]{1,0:T(8,128)(2,1)} %bitcast.10, bf16[256,2048]{1,0:T(8,128)(2,1)} %physical.1.refs_5_.advecting), custom_call_target="tpu_custom_call" | custom-call | flops 4294967296 | bytes 8388608 | tf_op jit(solution)/shard_map/products/pallas_call | solution.py:132
  122.4 3.9 %all-to-all-done.1.refs_5_.x = bf16[8,128,512]{2,1,0:T(8,128)(2,1)S(1)} async-done(((bf16[8,128,512]{2,1,0:T(8,128)(2,1)}), bf16[8,128,512]{2,1,0:T(8,128)(2,1)S(1)}, u32[]{:S(2)}, u32[]{:S(2)}) %all-to-all-start.1) | async-done | bytes 1048608 | tf_op jit(solution)/shard_map/all_to_all | solution.py:306
  126.3 3.6 %all-to-all-start.6 = ((bf16[8,128,512]{2,1,0:T(8,128)(2,1)}), bf16[8,128,512]{2,1,0:T(8,128)(2,1)S(1)}, u32[]{:S(2)}, u32[]{:S(2)}) async-start(bf16[8,128,512]{2,1,0:T(8,128)(2,1)} %products.5), calls=%async_computation.6 | async-start | bytes 2097152 | tf_op jit(solution)/shard_map/all_to_all | solution.py:306
  129.8 6.8 %collective-permute-done.1.refs_2_ = bf16[2,2,128,1024]{3,2,1,0:T(8,128)(2,1)} collective-permute-done((bf16[2,2,128,1024]{3,2,1,0:T(8,128)(2,1)S(1)}, bf16[2,2,128,1024]{3,2,1,0:T(8,128)(2,1)}, u32[]{:S(2)}, u32[]{:S(2)}) %collective-permute-start.1) | collective-permute-done | bytes 1048608 | tf_op jit(solution)/shard_map/ppermute | solution.py:288
  136.6 22.9 %collective-permute-done.refs_0_ = bf16[2,2,128,1024]{3,2,1,0:T(8,128)(2,1)} collective-permute-done((bf16[2,2,128,1024]{3,2,1,0:T(8,128)(2,1)S(1)}, bf16[2,2,128,1024]{3,2,1,0:T(8,128)(2,1)}, u32[]{:S(2)}, u32[]{:S(2)}) %collective-permute-start) | collective-permute-done | bytes 1048608 | tf_op jit(solution)/shard_map/ppermute | solution.py:287
  159.5 0.0 copy-done.3
  159.5 6.1 %radial.6 = bf16[8,128,512]{2,1,0:T(8,128)(2,1)} custom-call(bf16[2,2,128,1024]{3,2,1,0:T(8,128)(2,1)} %collective-permute-done.refs_0_, bf16[2,2,128,1024]{3,2,1,0:T(8,128)(2,1)} %split.6._.refs_1_, bf16[2,2,128,1024]{3,2,1,0:T(8,128)(2,1)} %collective-permute-done.1.refs_2_, f32[128,1024]{1,0:T(8,128)} %get-tuple-element.16.refs_1_.refs_3_, ...), custom_call_target="tpu_custom_call" | custom-call | flops 1073741824 | bytes 4194304 | tf_op jit(solution)/shard_map/radial/pallas_call | solution.py:218
  165.6 0.0 all-to-all-done.6.y
  165.6 3.8 %all-to-all-start.2 = ((bf16[8,128,512]{2,1,0:T(8,128)(2,1)}), bf16[8,128,512]{2,1,0:T(8,128)(2,1)S(1)}, u32[]{:S(2)}, u32[]{:S(2)}) async-start(bf16[8,128,512]{2,1,0:T(8,128)(2,1)} %radial.6), calls=%async_computation.2 | async-start | bytes 2097152 | tf_op jit(solution)/shard_map/all_to_all | solution.py:306
  169.4 9.4 %products.4 = bf16[8,128,512]{2,1,0:T(8,128)(2,1)} custom-call(bf16[8,128,512]{2,1,0:T(8,128)(2,1)} %copy-done.3, bf16[2048,2048]{1,0:T(8,128)(2,1)} %bitcast.11, bf16[256,2048]{1,0:T(8,128)(2,1)} %physical.1.refs_5_.advecting), custom_call_target="tpu_custom_call" | custom-call | flops 4294967296 | bytes 8388608 | tf_op jit(solution)/shard_map/products/pallas_call | solution.py:132
  178.8 6.0 %all-to-all-done.2.x = bf16[8,128,512]{2,1,0:T(8,128)(2,1)S(1)} async-done(((bf16[8,128,512]{2,1,0:T(8,128)(2,1)}), bf16[8,128,512]{2,1,0:T(8,128)(2,1)S(1)}, u32[]{:S(2)}, u32[]{:S(2)}) %all-to-all-start.2) | async-done | bytes 1048608 | tf_op jit(solution)/shard_map/all_to_all | solution.py:306
  184.8 3.8 %all-to-all-start.4 = ((bf16[8,128,512]{2,1,0:T(8,128)(2,1)}), bf16[8,128,512]{2,1,0:T(8,128)(2,1)S(1)}, u32[]{:S(2)}, u32[]{:S(2)}) async-start(bf16[8,128,512]{2,1,0:T(8,128)(2,1)} %products.4), calls=%async_computation.4 | async-start | bytes 2097152 | tf_op jit(solution)/shard_map/all_to_all | solution.py:306
  188.6 0.0 copy-done.9
  188.6 9.4 %products.3 = bf16[8,128,512]{2,1,0:T(8,128)(2,1)} custom-call(bf16[8,128,512]{2,1,0:T(8,128)(2,1)} %copy-done.9, bf16[2048,2048]{1,0:T(8,128)(2,1)} %bitcast.12, bf16[256,2048]{1,0:T(8,128)(2,1)} %physical.1.refs_5_.advecting), custom_call_target="tpu_custom_call" | custom-call | flops 4294967296 | bytes 8388608 | tf_op jit(solution)/shard_map/products/pallas_call | solution.py:132
  198.0 5.7 %all-to-all-done.4.y = bf16[8,128,512]{2,1,0:T(8,128)(2,1)S(1)} async-done(((bf16[8,128,512]{2,1,0:T(8,128)(2,1)}), bf16[8,128,512]{2,1,0:T(8,128)(2,1)S(1)}, u32[]{:S(2)}, u32[]{:S(2)}) %all-to-all-start.4) | async-done | bytes 1048608 | tf_op jit(solution)/shard_map/all_to_all | solution.py:306
  203.7 3.6 %all-to-all-start.3 = ((bf16[8,128,512]{2,1,0:T(8,128)(2,1)}), bf16[8,128,512]{2,1,0:T(8,128)(2,1)S(1)}, u32[]{:S(2)}, u32[]{:S(2)}) async-start(bf16[8,128,512]{2,1,0:T(8,128)(2,1)} %products.3), calls=%async_computation.3 | async-start | bytes 2097152 | tf_op jit(solution)/shard_map/all_to_all | solution.py:306
  207.2 6.0 %analysis.3.refs_0_ = bf16[3,2,128,2,1024]{4,3,2,1,0:T(2,128)(2,1)} custom-call(bf16[8,128,512]{2,1,0:T(8,128)(2,1)} %copy-done.6, bf16[1024,1024]{1,0:T(8,128)(2,1)} %bitcast.6, f32[128,1024]{1,0:T(8,128)} %get-tuple-element.15.kept), custom_call_target="tpu_custom_call" | custom-call | flops 1073741824 | bytes 2097152 | tf_op jit(solution)/shard_map/analysis/pallas_call | solution.py:252
  213.2 6.0 %analysis.4.refs_0_ = bf16[3,2,128,2,1024]{4,3,2,1,0:T(2,128)(2,1)} custom-call(bf16[8,128,512]{2,1,0:T(8,128)(2,1)} %copy-done.4, bf16[1024,1024]{1,0:T(8,128)(2,1)} %bitcast.7, f32[128,1024]{1,0:T(8,128)} %get-tuple-element.15.kept, bf16[3,2,128,2,1024]{4,3,2,1,0:T(2,128)(2,1)} %analysis.3.refs_0_), custom_call_target="tpu_custom_call", output_to_operand_aliasing={{}: (3, {})} | custom-call | flops 1073741824 | bytes 2097152 | tf_op jit(solution)/shard_map/analysis/pallas_call | solution.py:252
  219.2 3.4 %all-to-all-done.3.y = bf16[8,128,512]{2,1,0:T(8,128)(2,1)S(1)} async-done(((bf16[8,128,512]{2,1,0:T(8,128)(2,1)}), bf16[8,128,512]{2,1,0:T(8,128)(2,1)S(1)}, u32[]{:S(2)}, u32[]{:S(2)}) %all-to-all-start.3) | async-done | bytes 1048608 | tf_op jit(solution)/shard_map/all_to_all | solution.py:306
  222.6 1.0 copy-done.5
  223.5 6.0 %analysis.5 = bf16[3,2,128,2,1024]{4,3,2,1,0:T(2,128)(2,1)} custom-call(bf16[8,128,512]{2,1,0:T(8,128)(2,1)} %copy-done.5, bf16[1024,1024]{1,0:T(8,128)(2,1)} %bitcast.8, f32[128,1024]{1,0:T(8,128)} %get-tuple-element.15.kept, bf16[3,2,128,2,1024]{4,3,2,1,0:T(2,128)(2,1)} %analysis.4.refs_0_), custom_call_target="tpu_custom_call", output_to_operand_aliasing={{}: (3, {})} | custom-call | flops 1073741824 | bytes 2097152 | tf_op jit(solution)/shard_map/analysis/pallas_call | solution.py:252
  (17 shorter events, 0.0 us)
Async XLA Ops:
  0.0 17.0 %copy-start.11 = (s32[1024]{0:T(1024)S(1)}, s32[1024]{0:T(1024)}, u32[]{:S(2)}) copy-start(s32[1024]{0:T(1024)} %param.5) | copy-start | bytes 12292
  4.8 59.5 %collective-permute-start.5 = (bf16[2,2,128,1024]{3,2,1,0:T(8,128)(2,1)}, bf16[2,2,128,1024]{3,2,1,0:T(8,128)(2,1)S(1)}, u32[]{:S(2)}, u32[]{:S(2)}) collective-permute-start(bf16[2,2,128,1024]{3,2,1,0:T(8,128)(2,1)} %split.4._.refs_1_), channel_id=1, source_target_pairs={{1,0},{2,1},{3,2},{0,3},{5,4},{6,5},{7,6},{4,7},{9,8},{10,9},{11,1... | collective-permute-start | bytes 3145736 | tf_op jit(solution)/shard_map/ppermute | solution.py:288
  9.9 54.5 %collective-permute-start.4 = (bf16[2,2,128,1024]{3,2,1,0:T(8,128)(2,1)}, bf16[2,2,128,1024]{3,2,1,0:T(8,128)(2,1)}, u32[]{:S(2)}, u32[]{:S(2)}) collective-permute-start(bf16[2,2,128,1024]{3,2,1,0:T(8,128)(2,1)} %split.4._.refs_1_), channel_id=1, source_target_pairs={{0,1},{1,2},{2,3},{3,0},{4,5},{5,6},{6,7},{7,4},{8,9},{9,10},{10,1... | collective-permute-start | bytes 3145736 | tf_op jit(solution)/shard_map/ppermute | solution.py:287
  39.8 9.2 %copy-start.2 = (bf16[2,2,128,1024]{3,2,1,0:T(8,128)(2,1)S(1)}, bf16[2,2,128,1024]{3,2,1,0:T(8,128)(2,1)}, u32[]{:S(2)}) copy-start(bf16[2,2,128,1024]{3,2,1,0:T(8,128)(2,1)} %split.5._.refs_1_) | copy-start | bytes 3145732
  45.3 19.1 %all-to-all-start = ((bf16[8,128,512]{2,1,0:T(8,128)(2,1)}), bf16[8,128,512]{2,1,0:T(8,128)(2,1)S(1)}, u32[]{:S(2)}, u32[]{:S(2)}) async-start(bf16[8,128,512]{2,1,0:T(8,128)(2,1)} %radial.4), calls=%async_computation | async-start | bytes 2097152 | tf_op jit(solution)/shard_map/all_to_all | solution.py:306
  49.0 50.0 %collective-permute-start.3 = (bf16[2,2,128,1024]{3,2,1,0:T(8,128)(2,1)S(1)}, bf16[2,2,128,1024]{3,2,1,0:T(8,128)(2,1)}, u32[]{:S(2)}, u32[]{:S(2)}) collective-permute-start(bf16[2,2,128,1024]{3,2,1,0:T(8,128)(2,1)S(1)} %copy-done.2), channel_id=1, source_target_pairs={{1,0},{2,1},{3,2},{0,3},{5,4},{6,5},{7,6},{4,7},{9,8},{10,9},{11,1... | collective-permute-start | bytes 3145736 | tf_op jit(solution)/shard_map/ppermute | solution.py:288
  52.9 48.1 %collective-permute-start.2 = (bf16[2,2,128,1024]{3,2,1,0:T(8,128)(2,1)S(1)}, bf16[2,2,128,1024]{3,2,1,0:T(8,128)(2,1)}, u32[]{:S(2)}, u32[]{:S(2)}) collective-permute-start(bf16[2,2,128,1024]{3,2,1,0:T(8,128)(2,1)S(1)} %copy-done.2), channel_id=1, source_target_pairs={{0,1},{1,2},{2,3},{3,0},{4,5},{5,6},{6,7},{7,4},{8,9},{9,10},{10,1... | collective-permute-start | bytes 3145736 | tf_op jit(solution)/shard_map/ppermute | solution.py:287
  52.9 22.7 %copy-start.10 = (s32[1024]{0:T(1024)S(1)}, s32[1024]{0:T(1024)}, u32[]{:S(2)}) copy-start(s32[1024]{0:T(1024)} %refs_3_.1) | copy-start | bytes 12292
  64.4 1.0 copy-start
  64.4 1.3 copy-start.7
  71.8 35.3 %all-to-all-start.5 = ((bf16[8,128,512]{2,1,0:T(8,128)(2,1)}), bf16[8,128,512]{2,1,0:T(8,128)(2,1)S(1)}, u32[]{:S(2)}, u32[]{:S(2)}) async-start(bf16[8,128,512]{2,1,0:T(8,128)(2,1)} %radial.7), calls=%async_computation.5 | async-start | bytes 2097152 | tf_op jit(solution)/shard_map/all_to_all | solution.py:306
  99.0 11.9 %copy-start.1 = (bf16[2,2,128,1024]{3,2,1,0:T(8,128)(2,1)S(1)}, bf16[2,2,128,1024]{3,2,1,0:T(8,128)(2,1)}, u32[]{:S(2)}) copy-start(bf16[2,2,128,1024]{3,2,1,0:T(8,128)(2,1)} %split.6._.refs_1_) | copy-start | bytes 3145732
  107.2 5.9 %copy-start.8 = (bf16[8,128,512]{2,1,0:T(8,128)(2,1)}, bf16[8,128,512]{2,1,0:T(8,128)(2,1)S(1)}, u32[]{:S(2)}) copy-start(bf16[8,128,512]{2,1,0:T(8,128)(2,1)S(1)} %all-to-all-done.5.x) | copy-start | bytes 3145732
  107.2 19.1 %all-to-all-start.1 = ((bf16[8,128,512]{2,1,0:T(8,128)(2,1)}), bf16[8,128,512]{2,1,0:T(8,128)(2,1)S(1)}, u32[]{:S(2)}, u32[]{:S(2)}) async-start(bf16[8,128,512]{2,1,0:T(8,128)(2,1)} %radial.5), calls=%async_computation.1 | async-start | bytes 2097152 | tf_op jit(solution)/shard_map/all_to_all | solution.py:306
  110.9 25.7 %collective-permute-start.1 = (bf16[2,2,128,1024]{3,2,1,0:T(8,128)(2,1)S(1)}, bf16[2,2,128,1024]{3,2,1,0:T(8,128)(2,1)}, u32[]{:S(2)}, u32[]{:S(2)}) collective-permute-start(bf16[2,2,128,1024]{3,2,1,0:T(8,128)(2,1)S(1)} %copy-done.1), channel_id=1, source_target_pairs={{1,0},{2,1},{3,2},{0,3},{5,4},{6,5},{7,6},{4,7},{9,8},{10,9},{11,1... | collective-permute-start | bytes 3145736 | tf_op jit(solution)/shard_map/ppermute | solution.py:288
  113.0 46.4 %collective-permute-start = (bf16[2,2,128,1024]{3,2,1,0:T(8,128)(2,1)S(1)}, bf16[2,2,128,1024]{3,2,1,0:T(8,128)(2,1)}, u32[]{:S(2)}, u32[]{:S(2)}) collective-permute-start(bf16[2,2,128,1024]{3,2,1,0:T(8,128)(2,1)S(1)} %copy-done.1), channel_id=1, source_target_pairs={{0,1},{1,2},{2,3},{3,0},{4,5},{5,6},{6,7},{7,4},{8,9},{9,10},{10,1... | collective-permute-start | bytes 3145736 | tf_op jit(solution)/shard_map/ppermute | solution.py:287
  126.3 33.2 %copy-start.3 = (bf16[8,128,512]{2,1,0:T(8,128)(2,1)}, bf16[8,128,512]{2,1,0:T(8,128)(2,1)S(1)}, u32[]{:S(2)}) copy-start(bf16[8,128,512]{2,1,0:T(8,128)(2,1)S(1)} %all-to-all-done.1.refs_5_.x) | copy-start | bytes 3145732
  126.3 39.4 %all-to-all-start.6 = ((bf16[8,128,512]{2,1,0:T(8,128)(2,1)}), bf16[8,128,512]{2,1,0:T(8,128)(2,1)S(1)}, u32[]{:S(2)}, u32[]{:S(2)}) async-start(bf16[8,128,512]{2,1,0:T(8,128)(2,1)} %products.5), calls=%async_computation.6 | async-start | bytes 2097152 | tf_op jit(solution)/shard_map/all_to_all | solution.py:306
  165.6 13.2 %copy-start.6 = (bf16[8,128,512]{2,1,0:T(8,128)(2,1)}, bf16[8,128,512]{2,1,0:T(8,128)(2,1)S(1)}, u32[]{:S(2)}) copy-start(bf16[8,128,512]{2,1,0:T(8,128)(2,1)S(1)} %all-to-all-done.6.y) | copy-start | bytes 3145732
  165.6 19.2 %all-to-all-start.2 = ((bf16[8,128,512]{2,1,0:T(8,128)(2,1)}), bf16[8,128,512]{2,1,0:T(8,128)(2,1)S(1)}, u32[]{:S(2)}, u32[]{:S(2)}) async-start(bf16[8,128,512]{2,1,0:T(8,128)(2,1)} %radial.6), calls=%async_computation.2 | async-start | bytes 2097152 | tf_op jit(solution)/shard_map/all_to_all | solution.py:306
  184.8 3.8 %copy-start.9 = (bf16[8,128,512]{2,1,0:T(8,128)(2,1)}, bf16[8,128,512]{2,1,0:T(8,128)(2,1)S(1)}, u32[]{:S(2)}) copy-start(bf16[8,128,512]{2,1,0:T(8,128)(2,1)S(1)} %all-to-all-done.2.x) | copy-start | bytes 3145732
  184.8 18.9 %all-to-all-start.4 = ((bf16[8,128,512]{2,1,0:T(8,128)(2,1)}), bf16[8,128,512]{2,1,0:T(8,128)(2,1)S(1)}, u32[]{:S(2)}, u32[]{:S(2)}) async-start(bf16[8,128,512]{2,1,0:T(8,128)(2,1)} %products.4), calls=%async_computation.4 | async-start | bytes 2097152 | tf_op jit(solution)/shard_map/all_to_all | solution.py:306
  203.7 9.5 %copy-start.4 = (bf16[8,128,512]{2,1,0:T(8,128)(2,1)}, bf16[8,128,512]{2,1,0:T(8,128)(2,1)S(1)}, u32[]{:S(2)}) copy-start(bf16[8,128,512]{2,1,0:T(8,128)(2,1)S(1)} %all-to-all-done.4.y) | copy-start | bytes 3145732
  203.7 18.9 %all-to-all-start.3 = ((bf16[8,128,512]{2,1,0:T(8,128)(2,1)}), bf16[8,128,512]{2,1,0:T(8,128)(2,1)S(1)}, u32[]{:S(2)}, u32[]{:S(2)}) async-start(bf16[8,128,512]{2,1,0:T(8,128)(2,1)} %products.3), calls=%async_computation.3 | async-start | bytes 2097152 | tf_op jit(solution)/shard_map/all_to_all | solution.py:306
  222.6 1.0 copy-start.5
